TPU v7x, 32 devices: a whole 2x2x4 slice. The times are simulated.
32 devices in a mesh: groups: 2 (over y), seq: 8 (over z, x), vocab: 1, batch: 2 (over core).
Axes of the slice: x: 2, y: 2, z: 4, core: 2. Of those that a mesh axis runs over, the one named last changes fastest.
Arguments:
- queries: bfloat16 [4, 1536, 3584], P(('groups', 'vocab', 'batch'), 'seq'), parts along dimension 0, may hold values from -300 to 300
- keys: bfloat16 [4, 1536, 512], P(('groups', 'vocab', 'batch'), 'seq'), parts along dimension 0, may hold values from -10 to 10
- values: bfloat16 [4, 1536, 512], P(('groups', 'vocab', 'batch'), 'seq'), parts along dimension 0, may hold values from -24 to 24
- residual: bfloat16 [4, 1536, 3584], P(('groups', 'vocab', 'batch'), 'seq'), parts along dimension 0, may hold values from -2048 to 2048
- norm_gain: float32 [3584], replicated, may hold values from 0.5 to 1.5
Outputs:
- normed: bfloat16 [4, 1536, 3584], P(('groups', 'vocab', 'batch'), 'seq'), parts along dimension 0
There are 2 independent parts, one for each index of `groups`. A program takes and returns all parts, laid end to end along the dimension named above; an argument that names none is the same for every part. Nothing has to cross between parts.
All inputs are finite; a program needn't handle non-finite values.
Results may differ from a plain program's by a relative error of at most 0.0049.
Values may be sent and summed in bfloat16 or wider, within the bound.
A program may use at most 128 MiB of HBM per device.

v0:
```python
import functools
import math

import jax
import jax.numpy as jnp
from jax import lax
from jax.experimental import pallas as pl
from jax.experimental.pallas import tpu as pltpu
from jax.sharding import PartitionSpec as P

HEAD_WIDTH = 128
norm_eps = 1e-06
MESH = pl.DeviceIdType.MESH


def kernel(
    planes,
    rows,
    kv_heads,
    per_group,
    q_hbm,
    kv_hbm,
    r_hbm,
    gain_ref,
    out_ref,
    qbuf,
    rbuf,
    kvbuf,
    top,
    acc,
    squares,
    local_sem,
    own_sem,
    up_send,
    up_recv,
    side_send,
    side_recv,
    extra_send,
    extra_recv,
):
    W = HEAD_WIDTH
    width = kv_heads * per_group * W
    me = lax.axis_index("seq")
    plane = me // 2
    col = lax.rem(me, 2)
    above = me + 2
    below = me - 2
    side = me + 1 - 2 * col
    has_up = plane + 1 < planes
    has_down = plane > 0
    factor = math.log2(math.e) / math.sqrt(W)

    own = []
    for g in range(kv_heads):
        copy = pltpu.make_async_copy(kv_hbm.at[g], kvbuf.at[g, me], own_sem.at[g])
        copy.start()
        own.append(copy)
    heads = kv_heads * per_group

    def query_copy(head):
        lanes = pl.ds(pl.multiple_of(head * W, W), W)
        return pltpu.make_async_copy(
            q_hbm.at[0, :, lanes], qbuf.at[head], local_sem.at[head]
        )

    r_in = pltpu.make_async_copy(r_hbm.at[0], rbuf, local_sem.at[heads])

    barrier = pltpu.get_barrier_semaphore()
    pl.semaphore_signal(barrier, inc=1, device_id={"seq": side}, device_id_type=MESH)

    @pl.when(has_up)
    def _():
        pl.semaphore_signal(barrier, inc=1, device_id={"seq": above}, device_id_type=MESH)

    @pl.when(has_down)
    def _():
        pl.semaphore_signal(barrier, inc=1, device_id={"seq": below}, device_id_type=MESH)

    pl.semaphore_wait(barrier, 1 + has_up.astype(jnp.int32) + has_down.astype(jnp.int32))

    def remote(slot, send_sem, recv_sem, target):
        return pltpu.make_async_remote_copy(
            src_ref=slot,
            dst_ref=slot,
            send_sem=send_sem,
            recv_sem=recv_sem,
            device_id={"seq": target},
            device_id_type=MESH,
        )

    def up_copy(g, q):
        return remote(kvbuf.at[g, 2 * q + col], up_send.at[g, q], up_recv.at[g, q], above)

    def side_copy(g, q, column):
        return remote(kvbuf.at[g, 2 * q + column], side_send.at[g, q], side_recv.at[g, q], side)

    def extra_copy(g):
        return remote(kvbuf.at[g, 0], extra_send.at[g], extra_recv.at[g], above)

    def by_extra(g, q, column):
        return (column == 1) & (q == 0) & has_down & (lax.rem(g, 2) == 1)

    for g in range(kv_heads):
        own[g].wait()

        @pl.when(has_up)
        def _(g=g):
            up_copy(g, plane).start()

        @pl.when(col == 0)
        def _(g=g):
            side_copy(g, plane, col).start()

    lax.fori_loop(0, heads, lambda head, carry: query_copy(head).start(), None)
    r_in.start()

    @pl.when(col == 0)
    def _():
        for g in range(kv_heads):
            kvbuf[g, me + 1] = jnp.zeros((rows, 2 * W), jnp.bfloat16)

    squares[...] = jnp.zeros_like(squares)
    lax.fori_loop(0, heads, lambda head, carry: query_copy(head).wait(), None)
    r_in.wait()

    def relay(g, q):
        up_copy(g, q).wait_recv()

        @pl.when(has_up)
        def _():
            up_copy(g, q).start()

        @pl.when(jnp.logical_not(by_extra(g, q, 1 - col)))
        def _():
            side_copy(g, q, col).start()

    def attend(g, q, first):
        keys = kvbuf[g, pl.ds(2 * q, 2), :, :W].reshape(2 * rows, W)
        vals = kvbuf[g, pl.ds(2 * q, 2), :, W:].reshape(2 * rows, W)
        vals = jnp.concatenate([vals, jnp.ones_like(vals)], axis=1)

        def scores(j):
            return lax.dot_general(
                qbuf[g * per_group + j],
                keys,
                (((1,), (1,)), ((), ())),
                preferred_element_type=jnp.float32,
            )

        s_next = scores(0)
        for j in range(per_group):
            head = g * per_group + j
            s = s_next
            if j + 1 < per_group:
                s_next = scores(j + 1)
            if first:
                at_row = lax.broadcasted_iota(jnp.int32, s.shape, 0) + col * rows
                at_key = lax.broadcasted_iota(jnp.int32, s.shape, 1)
                s = jnp.where(at_key <= at_row, s, -jnp.inf)
            wide = jnp.broadcast_to(jnp.max(s, axis=1, keepdims=True), (rows, W))
            if not first:
                old = top[head]
                wide = jnp.maximum(old, wide)
            s = (s - jnp.concatenate([wide] * (2 * rows // W), axis=1)) * factor
            w = jnp.exp2(s).astype(jnp.bfloat16)
            o = jnp.dot(w, vals, preferred_element_type=jnp.float32)
            if not first:
                fade = jnp.exp2((old - wide) * factor)
                o = o + acc[head] * jnp.concatenate([fade, fade], axis=1)
            top[head] = wide
            acc[head] = o

    def finish(g):
        total = squares[...]
        for j in range(per_group):
            head = g * per_group + j
            lanes = pl.ds(pl.multiple_of(head * W, W), W)
            both = acc[head]
            attended = (both[:, :W] / both[:, W:]).astype(jnp.bfloat16).astype(jnp.float32)
            hidden = rbuf[:, lanes].astype(jnp.float32) + attended
            total = total + hidden * hidden
            top[head] = hidden
        squares[...] = total

    def diagonal(g, carry):
        @pl.when(has_down)
        def _():
            relay(g, plane - 1)

        @pl.when(col == 1)
        def _():
            side_copy(g, plane, 1 - col).wait_recv()

        @pl.when((col == 1) & (plane == 0) & has_up & (lax.rem(g, 2) == 1))
        def _():
            extra_copy(g).start()

        attend(g, plane, True)

        @pl.when(plane == 0)
        def _():
            finish(g)

        return carry

    lax.fori_loop(0, kv_heads, diagonal, 0)

    def step(t, carry):
        q = plane - t + 1

        def one(g, inner):
            @pl.when(t <= plane)
            def _():
                relay(g, q - 1)

            @pl.when(by_extra(g, q, col))
            def _():
                extra_copy(g).wait_recv()

            @pl.when(by_extra(g, q, col) & has_up)
            def _():
                extra_copy(g).start()

            @pl.when(jnp.logical_not(by_extra(g, q, col)))
            def _():
                side_copy(g, q, 1 - col).wait_recv()

            attend(g, q, False)

            @pl.when(q == 0)
            def _():
                finish(g)

            return inner

        return lax.fori_loop(0, kv_heads, one, carry)

    lax.fori_loop(2, plane + 2, step, 0)

    mean = jnp.sum(squares[...], axis=1, keepdims=True) / width
    scale = jnp.broadcast_to(lax.rsqrt(mean + norm_eps), (rows, W))
    for head in range(kv_heads * per_group):
        lanes = slice(head * W, (head + 1) * W)
        gain = gain_ref[lanes].reshape(1, W)
        out_ref[0, :, lanes] = (top[head] * scale * gain).astype(jnp.bfloat16)

    def drain_own(g, carry):
        @pl.when(has_up)
        def _():
            up_copy(g, plane).wait_send()

        @pl.when(col == 0)
        def _():
            side_copy(g, plane, col).wait_send()

        @pl.when((col == 1) & has_up & (lax.rem(g, 2) == 1))
        def _():
            extra_copy(g).wait_send()

        return carry

    lax.fori_loop(0, kv_heads, drain_own, 0)

    def drain(q, carry):
        def one(g, inner):
            @pl.when(has_up)
            def _():
                up_copy(g, q).wait_send()

            @pl.when(jnp.logical_not(by_extra(g, q, 1 - col)))
            def _():
                side_copy(g, q, col).wait_send()

            return inner

        return lax.fori_loop(0, kv_heads, one, carry)

    lax.fori_loop(0, plane, drain, 0)


def body(queries, keys, values, residual, norm_gain):
    count = lax.axis_size("seq")
    rows = queries.shape[1]
    width = queries.shape[2]
    kv_heads = keys.shape[2] // HEAD_WIDTH
    heads = width // HEAD_WIDTH
    planes = count // 2
    pairs = jnp.stack(
        [
            jnp.concatenate([x[0, :, g * HEAD_WIDTH : (g + 1) * HEAD_WIDTH] for x in (keys, values)], axis=1)
            for g in range(kv_heads)
        ]
    )
    hbm = pl.BlockSpec(memory_space=pltpu.HBM)
    vmem = pl.BlockSpec(memory_space=pltpu.VMEM)
    return pl.pallas_call(
        functools.partial(kernel, planes, rows, kv_heads, heads // kv_heads),
        out_shape=jax.ShapeDtypeStruct(queries.shape, jnp.bfloat16),
        in_specs=[hbm, hbm, hbm, vmem],
        out_specs=vmem,
        scratch_shapes=[
            pltpu.VMEM((heads, rows, HEAD_WIDTH), jnp.bfloat16),
            pltpu.VMEM((rows, width), jnp.bfloat16),
            pltpu.VMEM((kv_heads, count, rows, 2 * HEAD_WIDTH), jnp.bfloat16),
            pltpu.VMEM((heads, rows, HEAD_WIDTH), jnp.float32),
            pltpu.VMEM((heads, rows, 2 * HEAD_WIDTH), jnp.float32),
            pltpu.VMEM((rows, HEAD_WIDTH), jnp.float32),
            pltpu.SemaphoreType.DMA((heads + 1,)),
            pltpu.SemaphoreType.DMA((kv_heads,)),
            pltpu.SemaphoreType.DMA((kv_heads, planes)),
            pltpu.SemaphoreType.DMA((kv_heads, planes)),
            pltpu.SemaphoreType.DMA((kv_heads, planes)),
            pltpu.SemaphoreType.DMA((kv_heads, planes)),
            pltpu.SemaphoreType.DMA((kv_heads,)),
            pltpu.SemaphoreType.DMA((kv_heads,)),
        ],
        compiler_params=pltpu.CompilerParams(
            collective_id=0, has_side_effects=True, vmem_limit_bytes=54500000
        ),
    )(queries, pairs, residual, norm_gain)


def solution(mesh):
    rows = P(("groups", "vocab", "batch"), "seq", None)
    return jax.shard_map(
        body,
        mesh=mesh,
        in_specs=(rows, rows, rows, rows, P()),
        out_specs=rows,
        check_vma=False,
    )
```

profile of v0, /device:TPU:26, one launch (start us, length us, event | category | flops | bytes accessed | tf_op | source)
XLA Modules:
  0.0 42.0 jit_solution(12914597102797522768)
XLA Ops:
  0.0 0.0 copy-start
  0.0 0.9 %slice_bitcast_fusion.7 = (bf16[192,128]{1,0:T(8,128)(2,1)S(1)}, bf16[192,128]{1,0:T(8,128)(2,1)S(1)}, bf16[192,128]{1,0:T(8,128)(2,1)S(1)}, bf16[192,128]{1,0:T(8,128)(2,1)S(1)}) fusion(bf16[1,192,512]{2,1,0:T(8,128)(2,1)} %param.6), kind=kLoop, calls=%fused_computation.12 | loop fusion | bytes 393216 | tf_op jit(solution)/shard_map/squeeze | solution.py:290
  0.9 0.9 %slice_bitcast_fusion.6 = (bf16[192,128]{1,0:T(8,128)(2,1)S(1)}, bf16[192,128]{1,0:T(8,128)(2,1)S(1)}, bf16[192,128]{1,0:T(8,128)(2,1)S(1)}, bf16[192,128]{1,0:T(8,128)(2,1)S(1)}) fusion(bf16[1,192,512]{2,1,0:T(8,128)(2,1)} %param.7), kind=kLoop, calls=%fused_computation.11 | loop fusion | bytes 393216 | tf_op jit(solution)/shard_map/squeeze | solution.py:290
  1.9 0.1 pad_maximum_fusion.kv_hbm
  1.9 0.0 copy-done
  1.9 39.0 %shard_map.55 = bf16[1,192,3584]{2,1,0:T(8,128)(2,1)S(1)} custom-call(bf16[1,192,3584]{2,1,0:T(8,128)(2,1)} %q_hbm.1, bf16[4,192,256]{2,1,0:T(8,128)(2,1)S(1)} %pad_maximum_fusion.kv_hbm, bf16[1,192,3584]{2,1,0:T(8,128)(2,1)} %r_hbm.1, f32[3584]{0:T(1024)S(1)} %copy-done), custom_call_target="tpu_custom_call" | custom-call | tf_op jit(solution)/shard_map/pallas_call | solution.py:296
  41.0 1.1 %copy.7 = bf16[1,192,3584]{2,1,0:T(8,128)(2,1)} copy(bf16[1,192,3584]{2,1,0:T(8,128)(2,1)S(1)} %shard_map.55) | data formatting | bytes 2752512
  (2 shorter events, 0.1 us)
Async XLA Ops:
  0.0 1.9 %copy-start = (f32[3584]{0:T(1024)S(1)}, f32[3584]{0:T(1024)}, u32[]{:S(2)}) copy-start(f32[3584]{0:T(1024)} %gain_ref.1) | copy-start | bytes 43012
where the time goes:
time: 42.3 us; the launch traced here: 42 us
  Pallas kernels  39 us (92%)
  local copies, waits for them, and re-layouts  2.88 us (7%)
    pallas_call x1, Pallas kernels, body(): pl.pallas_call(functools.partial(kernel, planes, rows, kv_heads, heads //...  39 us
    squeeze x2, local copies, waits for them, and re-layouts, body(): x[0, :, g * HEAD_WIDTH:(g + 1) * HEAD_WIDTH]  1.79 us
    unnamed x3, local copies, waits for them, and re-layouts  1.08 us

commit v1 on v0

--- a/solution.py
+++ b/solution.py
@@ -19,10 +19,12 @@
     kv_heads,
     per_group,
     q_hbm,
-    kv_hbm,
+    k_hbm,
+    v_hbm,
     r_hbm,
+    gain_hbm,
+    out_ref,
     gain_ref,
-    out_ref,
     qbuf,
     rbuf,
     kvbuf,
@@ -39,7 +41,8 @@
     extra_recv,
 ):
     W = HEAD_WIDTH
-    width = kv_heads * per_group * W
+    heads = kv_heads * per_group
+    width = heads * W
     me = lax.axis_index("seq")
     plane = me // 2
     col = lax.rem(me, 2)
@@ -50,12 +53,28 @@
     has_down = plane > 0
     factor = math.log2(math.e) / math.sqrt(W)
 
+    barrier = pltpu.get_barrier_semaphore()
+
+    @pl.when(has_down)
+    def _():
+        pl.semaphore_signal(barrier, inc=1, device_id={"seq": below}, device_id_type=MESH)
+
+    pl.semaphore_signal(barrier, inc=1, device_id={"seq": side}, device_id_type=MESH)
+
+    @pl.when(has_up)
+    def _():
+        pl.semaphore_signal(barrier, inc=1, device_id={"seq": above}, device_id_type=MESH)
+
     own = []
     for g in range(kv_heads):
-        copy = pltpu.make_async_copy(kv_hbm.at[g], kvbuf.at[g, me], own_sem.at[g])
-        copy.start()
-        own.append(copy)
-    heads = kv_heads * per_group
+        lanes = slice(g * W, (g + 1) * W)
+        pair = (
+            pltpu.make_async_copy(k_hbm.at[0, :, lanes], kvbuf.at[g, me, :, :W], own_sem.at[g, 0]),
+            pltpu.make_async_copy(v_hbm.at[0, :, lanes], kvbuf.at[g, me, :, W:], own_sem.at[g, 1]),
+        )
+        for copy in pair:
+            copy.start()
+        own.append(pair)
 
     def query_copy(head):
         lanes = pl.ds(pl.multiple_of(head * W, W), W)
@@ -64,17 +83,10 @@
         )
 
     r_in = pltpu.make_async_copy(r_hbm.at[0], rbuf, local_sem.at[heads])
-
-    barrier = pltpu.get_barrier_semaphore()
-    pl.semaphore_signal(barrier, inc=1, device_id={"seq": side}, device_id_type=MESH)
-
-    @pl.when(has_up)
-    def _():
-        pl.semaphore_signal(barrier, inc=1, device_id={"seq": above}, device_id_type=MESH)
-
-    @pl.when(has_down)
-    def _():
-        pl.semaphore_signal(barrier, inc=1, device_id={"seq": below}, device_id_type=MESH)
+    lax.fori_loop(0, heads, lambda head, carry: query_copy(head).start(), None)
+    g_in = pltpu.make_async_copy(gain_hbm, gain_ref, local_sem.at[heads + 1])
+    r_in.start()
+    g_in.start()
 
     pl.semaphore_wait(barrier, 1 + has_up.astype(jnp.int32) + has_down.astype(jnp.int32))
 
@@ -101,7 +113,8 @@
         return (column == 1) & (q == 0) & has_down & (lax.rem(g, 2) == 1)
 
     for g in range(kv_heads):
-        own[g].wait()
+        for copy in own[g]:
+            copy.wait()
 
         @pl.when(has_up)
         def _(g=g):
@@ -111,17 +124,7 @@
         def _(g=g):
             side_copy(g, plane, col).start()
 
-    lax.fori_loop(0, heads, lambda head, carry: query_copy(head).start(), None)
-    r_in.start()
-
-    @pl.when(col == 0)
-    def _():
-        for g in range(kv_heads):
-            kvbuf[g, me + 1] = jnp.zeros((rows, 2 * W), jnp.bfloat16)
-
     squares[...] = jnp.zeros_like(squares)
-    lax.fori_loop(0, heads, lambda head, carry: query_copy(head).wait(), None)
-    r_in.wait()
 
     def relay(g, q):
         up_copy(g, q).wait_recv()
@@ -134,10 +137,11 @@
         def _():
             side_copy(g, q, col).start()
 
-    def attend(g, q, first):
-        keys = kvbuf[g, pl.ds(2 * q, 2), :, :W].reshape(2 * rows, W)
-        vals = kvbuf[g, pl.ds(2 * q, 2), :, W:].reshape(2 * rows, W)
+    def attend(g, blocks, first):
+        keys = jnp.concatenate([kvbuf[g, b, :, :W] for b in blocks], axis=0)
+        vals = jnp.concatenate([kvbuf[g, b, :, W:] for b in blocks], axis=0)
         vals = jnp.concatenate([vals, jnp.ones_like(vals)], axis=1)
+        size = len(blocks) * rows
 
         def scores(j):
             return lax.dot_general(
@@ -147,6 +151,10 @@
                 preferred_element_type=jnp.float32,
             )
 
+        def spread(x):
+            tail = [x[:, : size % W]] if size % W else []
+            return jnp.concatenate([x] * (size // W) + tail, axis=1)
+
         s_next = scores(0)
         for j in range(per_group):
             head = g * per_group + j
@@ -154,14 +162,14 @@
             if j + 1 < per_group:
                 s_next = scores(j + 1)
             if first:
-                at_row = lax.broadcasted_iota(jnp.int32, s.shape, 0) + col * rows
+                at_row = lax.broadcasted_iota(jnp.int32, s.shape, 0)
                 at_key = lax.broadcasted_iota(jnp.int32, s.shape, 1)
                 s = jnp.where(at_key <= at_row, s, -jnp.inf)
             wide = jnp.broadcast_to(jnp.max(s, axis=1, keepdims=True), (rows, W))
             if not first:
                 old = top[head]
                 wide = jnp.maximum(old, wide)
-            s = (s - jnp.concatenate([wide] * (2 * rows // W), axis=1)) * factor
+            s = (s - spread(wide)) * factor
             w = jnp.exp2(s).astype(jnp.bfloat16)
             o = jnp.dot(w, vals, preferred_element_type=jnp.float32)
             if not first:
@@ -183,59 +191,70 @@
         squares[...] = total
 
     def diagonal(g, carry):
-        @pl.when(has_down)
-        def _():
-            relay(g, plane - 1)
-
-        @pl.when(col == 1)
-        def _():
+        lax.fori_loop(0, per_group, lambda j, inner: query_copy(g * per_group + j).wait(), None)
+        attend(g, [me], True)
+        return carry
+
+    ahead = 2 * (1 - col)
+    pieces = plane * kv_heads
+
+    def relay_piece(i):
+        relay(lax.rem(i, kv_heads), plane - 1 - i // kv_heads)
+
+    lax.fori_loop(0, kv_heads, diagonal, 0)
+    r_in.wait()
+    g_in.wait()
+    lax.fori_loop(0, jnp.minimum(ahead, pieces), lambda i, carry: relay_piece(i), None)
+
+    @pl.when((col == 0) & (plane == 0))
+    def _():
+        lax.fori_loop(0, kv_heads, lambda g, carry: finish(g), None)
+
+    @pl.when((col == 1) & has_up & (plane == 0))
+    def _():
+        for g in range(1, kv_heads, 2):
             side_copy(g, plane, 1 - col).wait_recv()
-
-        @pl.when((col == 1) & (plane == 0) & has_up & (lax.rem(g, 2) == 1))
-        def _():
             extra_copy(g).start()
 
-        attend(g, plane, True)
-
-        @pl.when(plane == 0)
+    def step(i, carry):
+        g = lax.rem(i, kv_heads)
+        q = plane - 1 - i // kv_heads
+
+        @pl.when(i + ahead < pieces)
+        def _():
+            relay_piece(i + ahead)
+
+        side_copy(g, q + col, 1 - col).wait_recv()
+        attend(g, [2 * q + col, 2 * q + 1 + col], False)
+
+        @pl.when((col == 0) & (q == 0))
         def _():
             finish(g)
 
         return carry
 
-    lax.fori_loop(0, kv_heads, diagonal, 0)
-
-    def step(t, carry):
-        q = plane - t + 1
-
-        def one(g, inner):
-            @pl.when(t <= plane)
-            def _():
-                relay(g, q - 1)
-
-            @pl.when(by_extra(g, q, col))
-            def _():
-                extra_copy(g).wait_recv()
-
-            @pl.when(by_extra(g, q, col) & has_up)
-            def _():
-                extra_copy(g).start()
-
-            @pl.when(jnp.logical_not(by_extra(g, q, col)))
-            def _():
-                side_copy(g, q, 1 - col).wait_recv()
-
-            attend(g, q, False)
-
-            @pl.when(q == 0)
-            def _():
-                finish(g)
-
-            return inner
-
-        return lax.fori_loop(0, kv_heads, one, carry)
-
-    lax.fori_loop(2, plane + 2, step, 0)
+    lax.fori_loop(0, pieces, step, 0)
+
+    def last(g, carry):
+        @pl.when(by_extra(g, 0, col))
+        def _():
+            extra_copy(g).wait_recv()
+
+        @pl.when(by_extra(g, 0, col) & has_up)
+        def _():
+            extra_copy(g).start()
+
+        @pl.when(jnp.logical_not(by_extra(g, 0, col)) & (has_down | (lax.rem(g, 2) == 0) | jnp.logical_not(has_up)))
+        def _():
+            side_copy(g, 0, 0).wait_recv()
+
+        attend(g, [0], False)
+        finish(g)
+        return carry
+
+    @pl.when(col == 1)
+    def _():
+        lax.fori_loop(0, kv_heads, last, 0)
 
     mean = jnp.sum(squares[...], axis=1, keepdims=True) / width
     scale = jnp.broadcast_to(lax.rsqrt(mean + norm_eps), (rows, W))
@@ -285,28 +304,27 @@
     kv_heads = keys.shape[2] // HEAD_WIDTH
     heads = width // HEAD_WIDTH
     planes = count // 2
-    pairs = jnp.stack(
-        [
-            jnp.concatenate([x[0, :, g * HEAD_WIDTH : (g + 1) * HEAD_WIDTH] for x in (keys, values)], axis=1)
-            for g in range(kv_heads)
-        ]
+    queries, keys, values, residual, norm_gain = (
+        pltpu.with_memory_space_constraint(x, pltpu.HBM)
+        for x in (queries, keys, values, residual, norm_gain)
     )
     hbm = pl.BlockSpec(memory_space=pltpu.HBM)
     vmem = pl.BlockSpec(memory_space=pltpu.VMEM)
     return pl.pallas_call(
         functools.partial(kernel, planes, rows, kv_heads, heads // kv_heads),
-        out_shape=jax.ShapeDtypeStruct(queries.shape, jnp.bfloat16),
-        in_specs=[hbm, hbm, hbm, vmem],
+        out_shape=pltpu.VMEM(queries.shape, jnp.bfloat16),
+        in_specs=[hbm] * 5,
         out_specs=vmem,
         scratch_shapes=[
+            pltpu.VMEM((width,), jnp.float32),
             pltpu.VMEM((heads, rows, HEAD_WIDTH), jnp.bfloat16),
             pltpu.VMEM((rows, width), jnp.bfloat16),
             pltpu.VMEM((kv_heads, count, rows, 2 * HEAD_WIDTH), jnp.bfloat16),
             pltpu.VMEM((heads, rows, HEAD_WIDTH), jnp.float32),
             pltpu.VMEM((heads, rows, 2 * HEAD_WIDTH), jnp.float32),
             pltpu.VMEM((rows, HEAD_WIDTH), jnp.float32),
-            pltpu.SemaphoreType.DMA((heads + 1,)),
-            pltpu.SemaphoreType.DMA((kv_heads,)),
+            pltpu.SemaphoreType.DMA((heads + 2,)),
+            pltpu.SemaphoreType.DMA((kv_heads, 2)),
             pltpu.SemaphoreType.DMA((kv_heads, planes)),
             pltpu.SemaphoreType.DMA((kv_heads, planes)),
             pltpu.SemaphoreType.DMA((kv_heads, planes)),
@@ -317,7 +335,7 @@
         compiler_params=pltpu.CompilerParams(
             collective_id=0, has_side_effects=True, vmem_limit_bytes=54500000
         ),
-    )(queries, pairs, residual, norm_gain)
+    )(queries, keys, values, residual, norm_gain)
 
 
 def solution(mesh):

time: 42.3 us -> 37.2 us (0.88)
  Pallas kernels: 39 us -> 35.9 us
  local copies, waits for them, and re-layouts: 2.88 us -> 1.08 us
    pallas_call x1, Pallas kernels: 39 us -> 35.9 us  [body(): pl.pallas_call(functools.partial(kernel, planes, rows, kv_heads, heads //...]
    squeeze x2 -> x0, local copies, waits for them, and re-layouts: 1.79 us -> none  [body(): x[0, :, g * HEAD_WIDTH:(g + 1) * HEAD_WIDTH]]
    unnamed x3 -> x1, local copies, waits for them, and re-layouts: 1.08 us -> 1.08 us
where the time goes in v1:
time: 37.2 us; the launch traced here: 37 us
  Pallas kernels  35.9 us (97%)
  local copies, waits for them, and re-layouts  1.08 us (3%)
    pallas_call x1, Pallas kernels, body(): pl.pallas_call(functools.partial(kernel, planes, rows, kv_heads, heads //...  35.9 us
    unnamed x1, local copies, waits for them, and re-layouts  1.08 us

profile of v1, /device:TPU:26, one launch (start us, length us, event | category | flops | bytes accessed | tf_op | source)
XLA Modules:
  0.0 37.0 jit_solution(5551280422310789795)
XLA Ops:
  0.0 35.9 %shard_map.55 = bf16[1,192,3584]{2,1,0:T(8,128)(2,1)S(1)} custom-call(bf16[1,192,3584]{2,1,0:T(8,128)(2,1)} %q_hbm.1, bf16[1,192,512]{2,1,0:T(8,128)(2,1)} %k_hbm.1, bf16[1,192,512]{2,1,0:T(8,128)(2,1)} %v_hbm.1, bf16[1,192,3584]{2,1,0:T(8,128)(2,1)} %r_hbm.1, f32[3584]{0:T(1024)} %gain_hbm.1), custom_call_target="tpu_custom_call" | custom-call | tf_op jit(solution)/shard_map/pallas_call | solution.py:313
  35.9 1.1 %copy.7 = bf16[1,192,3584]{2,1,0:T(8,128)(2,1)} copy(bf16[1,192,3584]{2,1,0:T(8,128)(2,1)S(1)} %shard_map.55) | data formatting | bytes 2752512

commit v2 on v1

--- a/solution.py
+++ b/solution.py
@@ -30,6 +30,8 @@
     kvbuf,
     top,
     acc,
+    obuf,
+    stat,
     squares,
     local_sem,
     own_sem,
@@ -37,8 +39,10 @@
     up_recv,
     side_send,
     side_recv,
-    extra_send,
-    extra_recv,
+    q3_send,
+    q3_recv,
+    o_send,
+    o_recv,
 ):
     W = HEAD_WIDTH
     heads = kv_heads * per_group
@@ -51,6 +55,9 @@
     side = me + 1 - 2 * col
     has_up = plane + 1 < planes
     has_down = plane > 0
+    is_top = (plane == planes - 1) & (planes > 1)
+    is_help = plane == planes - 2
+    skip = is_top.astype(jnp.int32)
     factor = math.log2(math.e) / math.sqrt(W)
 
     barrier = pltpu.get_barrier_semaphore()
@@ -106,38 +113,68 @@
     def side_copy(g, q, column):
         return remote(kvbuf.at[g, 2 * q + column], side_send.at[g, q], side_recv.at[g, q], side)
 
-    def extra_copy(g):
-        return remote(kvbuf.at[g, 0], extra_send.at[g], extra_recv.at[g], above)
-
-    def by_extra(g, q, column):
-        return (column == 1) & (q == 0) & has_down & (lax.rem(g, 2) == 1)
+    q3_copy = pltpu.make_async_remote_copy(
+        src_ref=qbuf.at[pl.ds(0, per_group)],
+        dst_ref=qbuf.at[pl.ds(heads, per_group)],
+        send_sem=q3_send,
+        recv_sem=q3_recv,
+        device_id={"seq": below},
+        device_id_type=MESH,
+    )
+
+    def o_copy(j):
+        return remote(obuf.at[j], o_send.at[j], o_recv.at[j], above)
+
+    stat_copy = remote(stat, o_send.at[per_group], o_recv.at[per_group], above)
+
+    def goes_up(g):
+        return has_up & jnp.logical_not(is_help & (g == 0))
 
     for g in range(kv_heads):
         for copy in own[g]:
             copy.wait()
 
-        @pl.when(has_up)
+        @pl.when(goes_up(g))
         def _(g=g):
             up_copy(g, plane).start()
 
-        @pl.when(col == 0)
+        late = is_help & has_down if g >= 2 else False
+
+        @pl.when((col == 0) & jnp.logical_not(late))
         def _(g=g):
             side_copy(g, plane, col).start()
 
+        if g == 0:
+
+            @pl.when((col == 1) & is_help)
+            def _():
+                side_copy(0, plane, col).start()
+
     squares[...] = jnp.zeros_like(squares)
 
     def relay(g, q):
         up_copy(g, q).wait_recv()
 
-        @pl.when(has_up)
+        @pl.when(goes_up(g))
         def _():
             up_copy(g, q).start()
 
-        @pl.when(jnp.logical_not(by_extra(g, q, 1 - col)))
+        paced = is_help & (col == 0)
+
+        @pl.when(jnp.logical_not(paced & (g >= 2) & (q >= 1)))
         def _():
             side_copy(g, q, col).start()
 
-    def attend(g, blocks, first):
+        @pl.when(paced & (g < 2) & (q == plane - 1))
+        def _():
+            side_copy(g + 2, plane, col).start()
+
+        @pl.when(paced & (g == 0) & (q < plane - 1))
+        def _():
+            for h in range(2, kv_heads):
+                side_copy(h, q + 1, col).start()
+
+    def attend(base, g, blocks, first):
         keys = jnp.concatenate([kvbuf[g, b, :, :W] for b in blocks], axis=0)
         vals = jnp.concatenate([kvbuf[g, b, :, W:] for b in blocks], axis=0)
         vals = jnp.concatenate([vals, jnp.ones_like(vals)], axis=1)
@@ -145,7 +182,7 @@
 
         def scores(j):
             return lax.dot_general(
-                qbuf[g * per_group + j],
+                qbuf[base + j],
                 keys,
                 (((1,), (1,)), ((), ())),
                 preferred_element_type=jnp.float32,
@@ -157,7 +194,7 @@
 
         s_next = scores(0)
         for j in range(per_group):
-            head = g * per_group + j
+            head = base + j
             s = s_next
             if j + 1 < per_group:
                 s_next = scores(j + 1)
@@ -190,42 +227,120 @@
             top[head] = hidden
         squares[...] = total
 
+    def merge():
+        total = squares[...]
+        stat_copy.wait_recv()
+        pad = jnp.zeros((W - stat.shape[0], stat.shape[1]), jnp.float32)
+        far = jnp.transpose(jnp.concatenate([stat[...], pad], axis=0))[:rows]
+        for j in range(per_group):
+            lanes = slice(j * W, (j + 1) * W)
+            o_copy(j).wait_recv()
+            both = acc[j]
+            near = top[j] * factor + jnp.log(both[:, W:]) * math.log2(math.e)
+            share = 1.0 / (1.0 + jnp.exp2(near - jnp.broadcast_to(far[:, j : j + 1], (rows, W))))
+            mine = both[:, :W] / both[:, W:]
+            attended = mine + (obuf[j].astype(jnp.float32) - mine) * share
+            attended = attended.astype(jnp.bfloat16).astype(jnp.float32)
+            hidden = rbuf[:, lanes].astype(jnp.float32) + attended
+            total = total + hidden * hidden
+            top[j] = hidden
+        squares[...] = total
+
+    def emit():
+        lane = lax.broadcasted_iota(jnp.int32, (rows, W), 1)
+        far = jnp.zeros((rows, W), jnp.float32)
+        for j in range(per_group):
+            both = acc[heads + j]
+            total = top[heads + j] * factor + jnp.log(both[:, W:]) * math.log2(math.e)
+            far = jnp.where(lane == j, total, far)
+            obuf[j] = (both[:, :W] / both[:, W:]).astype(jnp.bfloat16)
+        pad = jnp.zeros((stat.shape[1] - rows, W), jnp.float32)
+        stat[...] = jnp.transpose(jnp.concatenate([far, pad], axis=0))[: stat.shape[0]]
+
+    def send_o():
+        stat_copy.start()
+        for j in range(per_group):
+            o_copy(j).start()
+
+    def helped(b, carry):
+        @pl.when(b == plane)
+        def _():
+            q3_copy.wait_recv()
+
+        @pl.when((b == plane) & ((col == 0) | (b == 0)))
+        def _():
+            side_copy(0, plane, 1 - col).wait_recv()
+
+        @pl.when((col == 1) & (b < plane) & ((b == 0) | (b == 1)))
+        def _():
+            side_copy(0, b, 0).wait_recv()
+
+        attend(heads, 0, [2 * b, 2 * b + 1], False)
+        return carry
+
     def diagonal(g, carry):
         lax.fori_loop(0, per_group, lambda j, inner: query_copy(g * per_group + j).wait(), None)
-        attend(g, [me], True)
+
+        @pl.when(is_top & (g == 0))
+        def _():
+            q3_copy.start()
+
+        attend(g * per_group, g, [me], True)
         return carry
 
-    ahead = 2 * (1 - col)
-    pieces = plane * kv_heads
+    ahead = jnp.where((col == 0) | is_help, 2, 0)
+    groups = kv_heads - skip
+    pieces = plane * groups
 
     def relay_piece(i):
-        relay(lax.rem(i, kv_heads), plane - 1 - i // kv_heads)
+        relay(lax.rem(i, groups) + skip, plane - 1 - i // groups)
 
     lax.fori_loop(0, kv_heads, diagonal, 0)
     r_in.wait()
     g_in.wait()
     lax.fori_loop(0, jnp.minimum(ahead, pieces), lambda i, carry: relay_piece(i), None)
 
+    @pl.when(is_help)
+    def _():
+        top[pl.ds(heads, per_group)] = jnp.full((per_group, rows, W), -1e30, jnp.float32)
+        acc[pl.ds(heads, per_group)] = jnp.zeros((per_group, rows, 2 * W), jnp.float32)
+
+    @pl.when(is_help & (plane == 0))
+    def _():
+        lax.fori_loop(0, 1, helped, 0)
+        emit()
+        send_o()
+
     @pl.when((col == 0) & (plane == 0))
     def _():
         lax.fori_loop(0, kv_heads, lambda g, carry: finish(g), None)
 
-    @pl.when((col == 1) & has_up & (plane == 0))
-    def _():
-        for g in range(1, kv_heads, 2):
-            side_copy(g, plane, 1 - col).wait_recv()
-            extra_copy(g).start()
-
     def step(i, carry):
-        g = lax.rem(i, kv_heads)
-        q = plane - 1 - i // kv_heads
-
-        @pl.when(i + ahead < pieces)
+        g = lax.rem(i, groups) + skip
+        q = plane - 1 - i // groups
+
+        @pl.when((i + ahead < pieces) & jnp.logical_not(is_help & (i + ahead == pieces - 1)))
         def _():
             relay_piece(i + ahead)
 
-        side_copy(g, q + col, 1 - col).wait_recv()
-        attend(g, [2 * q + col, 2 * q + 1 + col], False)
+        @pl.when(jnp.logical_not(is_help & (col == 1) & (q == 0) & (g == 0) & (plane > 1)))
+        def _():
+            side_copy(g, q + col, 1 - col).wait_recv()
+
+        final = is_help & (q == 0) & (g == 0)
+        whole = is_help & (g == kv_heads - 2) & (q >= 1)
+        second = is_help & (g == kv_heads - 1) & (q == 1)
+        low = jnp.where(whole, q + 1, jnp.where(second, 1, 0))
+        many = jnp.where(final, jnp.where(plane == 1, 2, 1), (whole | second).astype(jnp.int32))
+        lax.fori_loop(low, low + many, helped, 0)
+
+        @pl.when(final)
+        def _():
+            emit()
+            relay_piece(pieces - 1)
+            send_o()
+
+        attend(g * per_group, g, [2 * q + col, 2 * q + 1 + col], False)
 
         @pl.when((col == 0) & (q == 0))
         def _():
@@ -236,25 +351,27 @@
     lax.fori_loop(0, pieces, step, 0)
 
     def last(g, carry):
-        @pl.when(by_extra(g, 0, col))
-        def _():
-            extra_copy(g).wait_recv()
-
-        @pl.when(by_extra(g, 0, col) & has_up)
-        def _():
-            extra_copy(g).start()
-
-        @pl.when(jnp.logical_not(by_extra(g, 0, col)) & (has_down | (lax.rem(g, 2) == 0) | jnp.logical_not(has_up)))
-        def _():
-            side_copy(g, 0, 0).wait_recv()
-
-        attend(g, [0], False)
-        finish(g)
+        q = jnp.where(is_top & (g == 0), plane, 0)
+
+        @pl.when(jnp.logical_not(is_help & (g == 0)))
+        def _():
+            side_copy(g, q, 0).wait_recv()
+
+        attend(g * per_group, g, [2 * q], False)
+
+        @pl.when(jnp.logical_not(is_top & (g == 0)))
+        def _():
+            finish(g)
+
         return carry
 
     @pl.when(col == 1)
     def _():
         lax.fori_loop(0, kv_heads, last, 0)
+
+    @pl.when(is_top)
+    def _():
+        merge()
 
     mean = jnp.sum(squares[...], axis=1, keepdims=True) / width
     scale = jnp.broadcast_to(lax.rsqrt(mean + norm_eps), (rows, W))
@@ -264,17 +381,13 @@
         out_ref[0, :, lanes] = (top[head] * scale * gain).astype(jnp.bfloat16)
 
     def drain_own(g, carry):
-        @pl.when(has_up)
+        @pl.when(goes_up(g))
         def _():
             up_copy(g, plane).wait_send()
 
-        @pl.when(col == 0)
+        @pl.when((col == 0) | (is_help & (g == 0)))
         def _():
             side_copy(g, plane, col).wait_send()
-
-        @pl.when((col == 1) & has_up & (lax.rem(g, 2) == 1))
-        def _():
-            extra_copy(g).wait_send()
 
         return carry
 
@@ -282,19 +395,26 @@
 
     def drain(q, carry):
         def one(g, inner):
-            @pl.when(has_up)
+            @pl.when(goes_up(g))
             def _():
                 up_copy(g, q).wait_send()
 
-            @pl.when(jnp.logical_not(by_extra(g, q, 1 - col)))
-            def _():
-                side_copy(g, q, col).wait_send()
-
+            side_copy(g, q, col).wait_send()
             return inner
 
-        return lax.fori_loop(0, kv_heads, one, carry)
+        return lax.fori_loop(skip, kv_heads, one, carry)
 
     lax.fori_loop(0, plane, drain, 0)
+
+    @pl.when(is_top)
+    def _():
+        q3_copy.wait_send()
+
+    @pl.when(is_help)
+    def _():
+        stat_copy.wait_send()
+        for j in range(per_group):
+            o_copy(j).wait_send()
 
 
 def body(queries, keys, values, residual, norm_gain):
@@ -304,6 +424,7 @@
     kv_heads = keys.shape[2] // HEAD_WIDTH
     heads = width // HEAD_WIDTH
     planes = count // 2
+    per_group = heads // kv_heads
     queries, keys, values, residual, norm_gain = (
         pltpu.with_memory_space_constraint(x, pltpu.HBM)
         for x in (queries, keys, values, residual, norm_gain)
@@ -311,17 +432,19 @@
     hbm = pl.BlockSpec(memory_space=pltpu.HBM)
     vmem = pl.BlockSpec(memory_space=pltpu.VMEM)
     return pl.pallas_call(
-        functools.partial(kernel, planes, rows, kv_heads, heads // kv_heads),
+        functools.partial(kernel, planes, rows, kv_heads, per_group),
         out_shape=pltpu.VMEM(queries.shape, jnp.bfloat16),
         in_specs=[hbm] * 5,
         out_specs=vmem,
         scratch_shapes=[
             pltpu.VMEM((width,), jnp.float32),
-            pltpu.VMEM((heads, rows, HEAD_WIDTH), jnp.bfloat16),
+            pltpu.VMEM((heads + per_group, rows, HEAD_WIDTH), jnp.bfloat16),
             pltpu.VMEM((rows, width), jnp.bfloat16),
             pltpu.VMEM((kv_heads, count, rows, 2 * HEAD_WIDTH), jnp.bfloat16),
-            pltpu.VMEM((heads, rows, HEAD_WIDTH), jnp.float32),
-            pltpu.VMEM((heads, rows, 2 * HEAD_WIDTH), jnp.float32),
+            pltpu.VMEM((heads + per_group, rows, HEAD_WIDTH), jnp.float32),
+            pltpu.VMEM((heads + per_group, rows, 2 * HEAD_WIDTH), jnp.float32),
+            pltpu.VMEM((per_group, rows, HEAD_WIDTH), jnp.bfloat16),
+            pltpu.VMEM((-(-per_group // 8) * 8, -(-rows // HEAD_WIDTH) * HEAD_WIDTH), jnp.float32),
             pltpu.VMEM((rows, HEAD_WIDTH), jnp.float32),
             pltpu.SemaphoreType.DMA((heads + 2,)),
             pltpu.SemaphoreType.DMA((kv_heads, 2)),
@@ -329,8 +452,10 @@
             pltpu.SemaphoreType.DMA((kv_heads, planes)),
             pltpu.SemaphoreType.DMA((kv_heads, planes)),
             pltpu.SemaphoreType.DMA((kv_heads, planes)),
-            pltpu.SemaphoreType.DMA((kv_heads,)),
-            pltpu.SemaphoreType.DMA((kv_heads,)),
+            pltpu.SemaphoreType.DMA,
+            pltpu.SemaphoreType.DMA,
+            pltpu.SemaphoreType.DMA((per_group + 1,)),
+            pltpu.SemaphoreType.DMA((per_group + 1,)),
         ],
         compiler_params=pltpu.CompilerParams(
             collective_id=0, has_side_effects=True, vmem_limit_bytes=54500000

time: 37.2 us -> 35.1 us (0.944); the launches traced: 37 us -> 34.5 us
  Pallas kernels: 35.9 us -> 33.5 us
    pallas_call x1, Pallas kernels: 35.9 us -> 33.5 us  [body(): pl.pallas_call(functools.partial(kernel, planes, rows, kv_heads, per_grou...]
where the time goes in v2:
time: 35.1 us; the launch traced here: 34.5 us
  Pallas kernels  33.5 us (95%)
  local copies, waits for them, and re-layouts  1.08 us (3%)
    pallas_call x1, Pallas kernels, body(): pl.pallas_call(functools.partial(kernel, planes, rows, kv_heads, per_grou...  33.5 us
    unnamed x1, local copies, waits for them, and re-layouts  1.08 us

profile of v2, /device:TPU:26, one launch (start us, length us, event | category | flops | bytes accessed | tf_op | source)
XLA Modules:
  0.0 34.5 jit_solution(16781373463422647865)
XLA Ops:
  0.0 33.5 %shard_map.55 = bf16[1,192,3584]{2,1,0:T(8,128)(2,1)S(1)} custom-call(bf16[1,192,3584]{2,1,0:T(8,128)(2,1)} %q_hbm.1, bf16[1,192,512]{2,1,0:T(8,128)(2,1)} %k_hbm.1, bf16[1,192,512]{2,1,0:T(8,128)(2,1)} %v_hbm.1, bf16[1,192,3584]{2,1,0:T(8,128)(2,1)} %r_hbm.1, f32[3584]{0:T(1024)} %gain_hbm.1), custom_call_target="tpu_custom_call" | custom-call | tf_op jit(solution)/shard_map/pallas_call | solution.py:434
  33.5 1.1 %copy.7 = bf16[1,192,3584]{2,1,0:T(8,128)(2,1)} copy(bf16[1,192,3584]{2,1,0:T(8,128)(2,1)S(1)} %shard_map.55) | data formatting | bytes 2752512

commit v3 on v2

--- a/solution.py
+++ b/solution.py
@@ -43,6 +43,8 @@
     q3_recv,
     o_send,
     o_recv,
+    x_send,
+    x_recv,
 ):
     W = HEAD_WIDTH
     heads = kv_heads * per_group
@@ -113,6 +115,21 @@
     def side_copy(g, q, column):
         return remote(kvbuf.at[g, 2 * q + column], side_send.at[g, q], side_recv.at[g, q], side)
 
+    half = rows // 2
+    use_detour = planes > 3
+    detour_g = 1
+
+    def half_side(g, q):
+        slot = kvbuf.at[g, 2 * q, pl.ds(0, half)]
+        return remote(slot, side_send.at[g, q], side_recv.at[g, q], side)
+
+    def detour(q):
+        slot = kvbuf.at[detour_g, 2 * q, pl.ds(half, half)]
+        return remote(slot, x_send, x_recv, above)
+
+    def by_detour(g, q, column):
+        return use_detour & is_top & (q == plane - 2) & (g == detour_g) & (column == 0)
+
     q3_copy = pltpu.make_async_remote_copy(
         src_ref=qbuf.at[pl.ds(0, per_group)],
         dst_ref=qbuf.at[pl.ds(heads, per_group)],
@@ -150,6 +167,11 @@
             def _():
                 side_copy(0, plane, col).start()
 
+    @pl.when(is_top)
+    def _():
+        lax.fori_loop(0, per_group, lambda j, inner: query_copy(j).wait(), None)
+        q3_copy.start()
+
     squares[...] = jnp.zeros_like(squares)
 
     def relay(g, q):
@@ -161,7 +183,11 @@
 
         paced = is_help & (col == 0)
 
-        @pl.when(jnp.logical_not(paced & (g >= 2) & (q >= 1)))
+        @pl.when(by_detour(g, q, col))
+        def _():
+            half_side(g, q).start()
+
+        @pl.when(jnp.logical_not((paced & (g >= 2) & (q >= 1)) | by_detour(g, q, col)))
         def _():
             side_copy(g, q, col).start()
 
@@ -227,12 +253,13 @@
             top[head] = hidden
         squares[...] = total
 
-    def merge():
+    def merge(first, end):
         total = squares[...]
-        stat_copy.wait_recv()
+        if first == 0:
+            stat_copy.wait_recv()
         pad = jnp.zeros((W - stat.shape[0], stat.shape[1]), jnp.float32)
         far = jnp.transpose(jnp.concatenate([stat[...], pad], axis=0))[:rows]
-        for j in range(per_group):
+        for j in range(first, end):
             lanes = slice(j * W, (j + 1) * W)
             o_copy(j).wait_recv()
             both = acc[j]
@@ -279,11 +306,9 @@
         return carry
 
     def diagonal(g, carry):
-        lax.fori_loop(0, per_group, lambda j, inner: query_copy(g * per_group + j).wait(), None)
-
-        @pl.when(is_top & (g == 0))
-        def _():
-            q3_copy.start()
+        @pl.when(jnp.logical_not(is_top & (g == 0)))
+        def _():
+            lax.fori_loop(0, per_group, lambda j, inner: query_copy(g * per_group + j).wait(), None)
 
         attend(g * per_group, g, [me], True)
         return carry
@@ -315,6 +340,12 @@
     def _():
         lax.fori_loop(0, kv_heads, lambda g, carry: finish(g), None)
 
+    def paired(i, carry):
+        g = lax.rem(i, groups) + skip
+        q = plane - 1 - i // groups
+        attend(g * per_group, g, [2 * q + col, 2 * q + 1 + col], False)
+        return carry
+
     def step(i, carry):
         g = lax.rem(i, groups) + skip
         q = plane - 1 - i // groups
@@ -323,9 +354,23 @@
         def _():
             relay_piece(i + ahead)
 
-        @pl.when(jnp.logical_not(is_help & (col == 1) & (q == 0) & (g == 0) & (plane > 1)))
+        there = by_detour(g, q + col, 1 - col)
+
+        @pl.when(there)
+        def _():
+            half_side(g, q + col).wait_recv()
+            detour(q + col).wait_recv()
+
+        had = ((g == 0) & (q == 0) & (plane > 1)) | (use_detour & (g == detour_g) & (q == plane - 2))
+
+        @pl.when(jnp.logical_not((is_help & (col == 1) & had) | there))
         def _():
             side_copy(g, q + col, 1 - col).wait_recv()
+
+        @pl.when(use_detour & is_help & (col == 1) & (q == plane - 1) & (g == detour_g + 1))
+        def _():
+            side_copy(detour_g, q, 0).wait_recv()
+            detour(q).start()
 
         final = is_help & (q == 0) & (g == 0)
         whole = is_help & (g == kv_heads - 2) & (q >= 1)
@@ -340,7 +385,9 @@
             relay_piece(pieces - 1)
             send_o()
 
-        attend(g * per_group, g, [2 * q + col, 2 * q + 1 + col], False)
+        later = is_help & (q == 1) & (g == kv_heads - 1)
+        start = jnp.where(final & (plane > 1), i - 1, i)
+        lax.fori_loop(start, jnp.where(later, start, i + 1), paired, 0)
 
         @pl.when((col == 0) & (q == 0))
         def _():
@@ -349,10 +396,16 @@
         return carry
 
     lax.fori_loop(0, pieces, step, 0)
+
+    early = per_group - 2
 
     def last(g, carry):
         q = jnp.where(is_top & (g == 0), plane, 0)
 
+        @pl.when(is_top & (g == kv_heads - 1))
+        def _():
+            merge(0, early)
+
         @pl.when(jnp.logical_not(is_help & (g == 0)))
         def _():
             side_copy(g, q, 0).wait_recv()
@@ -369,9 +422,13 @@
     def _():
         lax.fori_loop(0, kv_heads, last, 0)
 
+    @pl.when(is_top & (col == 0))
+    def _():
+        merge(0, early)
+
     @pl.when(is_top)
     def _():
-        merge()
+        merge(early, per_group)
 
     mean = jnp.sum(squares[...], axis=1, keepdims=True) / width
     scale = jnp.broadcast_to(lax.rsqrt(mean + norm_eps), (rows, W))
@@ -399,7 +456,14 @@
             def _():
                 up_copy(g, q).wait_send()
 
-            side_copy(g, q, col).wait_send()
+            @pl.when(by_detour(g, q, col))
+            def _():
+                half_side(g, q).wait_send()
+
+            @pl.when(jnp.logical_not(by_detour(g, q, col)))
+            def _():
+                side_copy(g, q, col).wait_send()
+
             return inner
 
         return lax.fori_loop(skip, kv_heads, one, carry)
@@ -413,6 +477,11 @@
     @pl.when(is_help)
     def _():
         stat_copy.wait_send()
+
+        @pl.when(use_detour & (col == 1))
+        def _():
+            detour(plane - 1).wait_send()
+
         for j in range(per_group):
             o_copy(j).wait_send()
 
@@ -456,6 +525,8 @@
             pltpu.SemaphoreType.DMA,
             pltpu.SemaphoreType.DMA((per_group + 1,)),
             pltpu.SemaphoreType.DMA((per_group + 1,)),
+            pltpu.SemaphoreType.DMA,
+            pltpu.SemaphoreType.DMA,
         ],
         compiler_params=pltpu.CompilerParams(
             collective_id=0, has_side_effects=True, vmem_limit_bytes=54500000

time: 35.1 us -> 34.2 us (0.974)
  Pallas kernels: 33.5 us -> 32.7 us
    pallas_call x1, Pallas kernels: 33.5 us -> 32.7 us  [body(): pl.pallas_call(functools.partial(kernel, planes, rows, kv_heads, per_grou...]
where the time goes in v3:
time: 34.2 us; the launch traced here: 33.8 us
  Pallas kernels  32.7 us (96%)
  local copies, waits for them, and re-layouts  1.08 us (3%)
    pallas_call x1, Pallas kernels, body(): pl.pallas_call(functools.partial(kernel, planes, rows, kv_heads, per_grou...  32.7 us
    unnamed x1, local copies, waits for them, and re-layouts  1.08 us

profile of v3, /device:TPU:26, one launch (start us, length us, event | category | flops | bytes accessed | tf_op | source)
XLA Modules:
  0.0 33.8 jit_solution(8723097434362061816)
XLA Ops:
  0.0 32.7 %shard_map.55 = bf16[1,192,3584]{2,1,0:T(8,128)(2,1)S(1)} custom-call(bf16[1,192,3584]{2,1,0:T(8,128)(2,1)} %q_hbm.1, bf16[1,192,512]{2,1,0:T(8,128)(2,1)} %k_hbm.1, bf16[1,192,512]{2,1,0:T(8,128)(2,1)} %v_hbm.1, bf16[1,192,3584]{2,1,0:T(8,128)(2,1)} %r_hbm.1, f32[3584]{0:T(1024)} %gain_hbm.1), custom_call_target="tpu_custom_call" | custom-call | tf_op jit(solution)/shard_map/pallas_call | solution.py:503
  32.7 1.1 %copy.7 = bf16[1,192,3584]{2,1,0:T(8,128)(2,1)} copy(bf16[1,192,3584]{2,1,0:T(8,128)(2,1)S(1)} %shard_map.55) | data formatting | bytes 2752512

commit v4 on v3

--- a/solution.py
+++ b/solution.py
@@ -206,9 +206,12 @@
         vals = jnp.concatenate([vals, jnp.ones_like(vals)], axis=1)
         size = len(blocks) * rows
 
-        def scores(j):
+        packs = [(at, min(3, per_group - at)) for at in range(0, per_group, 3)]
+
+        def scores(k):
+            at, count = packs[k]
             return lax.dot_general(
-                qbuf[base + j],
+                qbuf[pl.ds(base + at, count)].reshape(count * rows, W),
                 keys,
                 (((1,), (1,)), ((), ())),
                 preferred_element_type=jnp.float32,
@@ -219,27 +222,28 @@
             return jnp.concatenate([x] * (size // W) + tail, axis=1)
 
         s_next = scores(0)
-        for j in range(per_group):
-            head = base + j
+        for k, (at, count) in enumerate(packs):
+            head = pl.ds(base + at, count)
+            tall = count * rows
             s = s_next
-            if j + 1 < per_group:
-                s_next = scores(j + 1)
+            if k + 1 < len(packs):
+                s_next = scores(k + 1)
             if first:
-                at_row = lax.broadcasted_iota(jnp.int32, s.shape, 0)
-                at_key = lax.broadcasted_iota(jnp.int32, s.shape, 1)
-                s = jnp.where(at_key <= at_row, s, -jnp.inf)
-            wide = jnp.broadcast_to(jnp.max(s, axis=1, keepdims=True), (rows, W))
+                at_row = lax.broadcasted_iota(jnp.int32, (rows, size), 0)
+                at_key = lax.broadcasted_iota(jnp.int32, (rows, size), 1)
+                s = jnp.where(jnp.concatenate([at_key <= at_row] * count, axis=0), s, -jnp.inf)
+            wide = jnp.broadcast_to(jnp.max(s, axis=1, keepdims=True), (tall, W))
             if not first:
-                old = top[head]
+                old = top[head].reshape(tall, W)
                 wide = jnp.maximum(old, wide)
             s = (s - spread(wide)) * factor
             w = jnp.exp2(s).astype(jnp.bfloat16)
             o = jnp.dot(w, vals, preferred_element_type=jnp.float32)
             if not first:
                 fade = jnp.exp2((old - wide) * factor)
-                o = o + acc[head] * jnp.concatenate([fade, fade], axis=1)
-            top[head] = wide
-            acc[head] = o
+                o = o + acc[head].reshape(tall, 2 * W) * jnp.concatenate([fade, fade], axis=1)
+            top[head] = wide.reshape(count, rows, W)
+            acc[head] = o.reshape(count, rows, 2 * W)
 
     def finish(g):
         total = squares[...]

time: 34.2 us -> 33.8 us (0.988)
  no operation moved by 1% of the time
where the time goes in v4:
time: 33.8 us; the launch traced here: 33.5 us
  Pallas kernels  32.4 us (96%)
  local copies, waits for them, and re-layouts  1.08 us (3%)
    pallas_call x1, Pallas kernels, body(): pl.pallas_call(functools.partial(kernel, planes, rows, kv_heads, per_grou...  32.4 us
    unnamed x1, local copies, waits for them, and re-layouts  1.08 us

profile of v4, /device:TPU:26, one launch (start us, length us, event | category | flops | bytes accessed | tf_op | source)
XLA Modules:
  0.0 33.5 jit_solution(15528906314034479865)
XLA Ops:
  0.0 32.4 %shard_map.55 = bf16[1,192,3584]{2,1,0:T(8,128)(2,1)S(1)} custom-call(bf16[1,192,3584]{2,1,0:T(8,128)(2,1)} %q_hbm.1, bf16[1,192,512]{2,1,0:T(8,128)(2,1)} %k_hbm.1, bf16[1,192,512]{2,1,0:T(8,128)(2,1)} %v_hbm.1, bf16[1,192,3584]{2,1,0:T(8,128)(2,1)} %r_hbm.1, f32[3584]{0:T(1024)} %gain_hbm.1), custom_call_target="tpu_custom_call" | custom-call | tf_op jit(solution)/shard_map/pallas_call | solution.py:507
  32.4 1.1 %copy.7 = bf16[1,192,3584]{2,1,0:T(8,128)(2,1)} copy(bf16[1,192,3584]{2,1,0:T(8,128)(2,1)S(1)} %shard_map.55) | data formatting | bytes 2752512

commit v5 on v4

--- a/solution.py
+++ b/solution.py
@@ -254,7 +254,7 @@
             attended = (both[:, :W] / both[:, W:]).astype(jnp.bfloat16).astype(jnp.float32)
             hidden = rbuf[:, lanes].astype(jnp.float32) + attended
             total = total + hidden * hidden
-            top[head] = hidden
+            top[head] = hidden * gain_ref[lanes].reshape(1, W)
         squares[...] = total
 
     def merge(first, end):
@@ -274,7 +274,7 @@
             attended = attended.astype(jnp.bfloat16).astype(jnp.float32)
             hidden = rbuf[:, lanes].astype(jnp.float32) + attended
             total = total + hidden * hidden
-            top[j] = hidden
+            top[j] = hidden * gain_ref[lanes].reshape(1, W)
         squares[...] = total
 
     def emit():
@@ -438,8 +438,7 @@
     scale = jnp.broadcast_to(lax.rsqrt(mean + norm_eps), (rows, W))
     for head in range(kv_heads * per_group):
         lanes = slice(head * W, (head + 1) * W)
-        gain = gain_ref[lanes].reshape(1, W)
-        out_ref[0, :, lanes] = (top[head] * scale * gain).astype(jnp.bfloat16)
+        out_ref[0, :, lanes] = (top[head] * scale).astype(jnp.bfloat16)
 
     def drain_own(g, carry):
         @pl.when(goes_up(g))

time: 33.8 us -> 33.7 us (level)
  no operation moved by 1% of the time
where the time goes in v5:
time: 33.7 us; the launch traced here: 33.5 us
  Pallas kernels  32.4 us (96%)
  local copies, waits for them, and re-layouts  1.08 us (3%)
    pallas_call x1, Pallas kernels, body(): pl.pallas_call(functools.partial(kernel, planes, rows, kv_heads, per_grou...  32.4 us
    unnamed x1, local copies, waits for them, and re-layouts  1.08 us

profile of v5, /device:TPU:26, one launch (start us, length us, event | category | flops | bytes accessed | tf_op | source)
XLA Modules:
  0.0 33.5 jit_solution(16320002212468414691)
XLA Ops:
  0.0 32.4 %shard_map.55 = bf16[1,192,3584]{2,1,0:T(8,128)(2,1)S(1)} custom-call(bf16[1,192,3584]{2,1,0:T(8,128)(2,1)} %q_hbm.1, bf16[1,192,512]{2,1,0:T(8,128)(2,1)} %k_hbm.1, bf16[1,192,512]{2,1,0:T(8,128)(2,1)} %v_hbm.1, bf16[1,192,3584]{2,1,0:T(8,128)(2,1)} %r_hbm.1, f32[3584]{0:T(1024)} %gain_hbm.1), custom_call_target="tpu_custom_call" | custom-call | tf_op jit(solution)/shard_map/pallas_call | solution.py:506
  32.4 1.1 %copy.7 = bf16[1,192,3584]{2,1,0:T(8,128)(2,1)} copy(bf16[1,192,3584]{2,1,0:T(8,128)(2,1)S(1)} %shard_map.55) | data formatting | bytes 2752512
